TPU v7x, 32 devices: a whole 2x2x4 slice. The times are simulated.
32 devices in a mesh: groups: 2 (over y), blk: 4 (over z), rep: 2 (over x), sub: 2 (over core).
Axes of the slice: x: 2, y: 2, z: 4, core: 2. Of those that a mesh axis runs over, the one named last changes fastest.
Arguments:
- replica_delta: bfloat16 [32, 32, 4608], P(('groups', 'blk', 'rep', 'sub')), parts along dimension 0, may hold values from -150 to 150
- momentum: float32 [64, 4608], P(('groups', 'blk')), parts along dimension 0, may hold values from -6 to 6
- params: float32 [64, 4608], P(('groups', 'blk')), parts along dimension 0, may hold values from -6 to 6
- prev_master: float32 [64, 4608], P(('groups', 'blk')), parts along dimension 0, may hold values from -6 to 6
Outputs:
- new_params: float32 [64, 4608], P(('groups', 'blk')), parts along dimension 0
- new_momentum: float32 [64, 4608], P(('groups', 'blk')), parts along dimension 0
- prev_weights: bfloat16 [64, 4608], P('groups'), parts along dimension 0
There are 2 independent parts, one for each index of `groups`. A program takes and returns all parts, laid end to end along the dimension named above; each array names one. Nothing has to cross between parts.
All inputs are finite; a program needn't handle non-finite values.
Results may differ from a plain program's by a relative error of at most 0.012.
Values may be sent and summed in bfloat16 or wider, within the bound.
No kernel may reach another device: no remote copies, remote signals or barrier semaphores. Data moves between devices by JAX's collectives and lax.ppermute only.
A program may use at most 64 MiB of HBM per device.

v0:
```python
import jax
import jax.numpy as jnp
from jax import lax
from jax.sharding import PartitionSpec as P

momentum_coef = 0.9
outer_rate = 0.7


def per_device(replica_delta, momentum, params, prev_master):
    own_delta = replica_delta[0]
    width = own_delta.shape[1]
    entries = own_delta.shape[0] * width
    share_sum = lax.psum_scatter(
        own_delta.astype(jnp.float32).astype(jnp.bfloat16), "blk", scatter_dimension=0, tiled=True
    )
    summed = lax.psum(share_sum, ("rep", "sub")).astype(jnp.float32)
    squares = lax.psum(jnp.sum(summed * summed), "blk")
    clip_factor = jnp.minimum(
        jnp.float32(1.0), jnp.sqrt(jnp.float32(entries)) / jnp.sqrt(squares + 1e-06)
    )
    scaled = clip_factor * summed
    new_momentum = momentum_coef * momentum + scaled
    new_params = params - outer_rate * (scaled + momentum_coef * new_momentum)
    prev_weights = lax.all_gather(prev_master.astype(jnp.bfloat16), "blk", axis=0, tiled=True)
    return (new_params, new_momentum, prev_weights)


def solution(mesh):
    in_specs = (
        P(("groups", "blk", "rep", "sub"), None, None),
        P(("groups", "blk"), None),
        P(("groups", "blk"), None),
        P(("groups", "blk"), None),
    )
    out_specs = (P(("groups", "blk"), None), P(("groups", "blk"), None), P("groups", None))
    return jax.shard_map(
        per_device, mesh=mesh, in_specs=in_specs, out_specs=out_specs, check_vma=False
    )
```

profile of v0, /device:TPU:0, one launch (start us, length us, event | category | flops | bytes accessed | tf_op | source)
XLA Modules:
  0.0 86.8 jit_solution(3447558341183904942)
XLA Ops:
  7.2 0.0 reduce-scatter.2.cloned.1.call-start
  7.2 0.0 copy-start.1
  7.2 0.7 reduce-scatter.2.cloned.1.call-update
  7.9 0.0 all-reduce.2.cloned.1.call-start
  7.9 0.2 copy-done.1
  8.1 25.1 %reduce-scatter.2.cloned.1.call-done = bf16[8,4608]{1,0:T(8,128)(2,1)} async-done(((bf16[32,4608]{1,0:T(8,128)(2,1)}), bf16[8,4608]{1,0:T(8,128)(2,1)}) %reduce-scatter.2.cloned.1.call-update) | async-done | bytes 73744 | tf_op jit(solution)/shard_map/reduce_scatter | solution.py:14
  33.2 0.0 all-reduce.2.cloned.1.call-update
  33.2 0.0 copy-start.2
  33.2 0.0 copy-start.3
  33.2 14.1 %all_gather.3 = bf16[32,4608]{1,0:T(8,128)(2,1)S(1)} all-gather(bf16[8,4608]{1,0:T(8,128)(2,1)S(1)} %convert_element_type.9), channel_id=1, replica_groups=mesh['groups'=2,'blk'=4,'rep'=2,'sub'=2] {'blk'}, dimensions={0}, use_global_device_ids=true | all-gather | bytes 368640 | tf_op jit(solution)/shard_map/all_gather | solution.py:25
  47.4 16.1 %all-reduce.2.cloned.1.call-done = bf16[8,4608]{1,0:T(8,128)(2,1)} async-done(((bf16[8,4608]{1,0:T(8,128)(2,1)}), bf16[8,4608]{1,0:T(8,128)(2,1)}) %all-reduce.2.cloned.1.call-update) | async-done | bytes 73744 | tf_op jit(solution)/shard_map/psum | solution.py:17
  63.5 0.0 copy-start
  63.5 1.6 %fusion.4 = f32[]{:T(128)} fusion(bf16[8,4608]{1,0:T(8,128)(2,1)} %all-reduce.2.cloned.1.call-done), kind=kLoop, calls=%fused_computation.6 | loop fusion | flops 110591 | bytes 73732 | tf_op jit(solution)/shard_map/reduce_sum | solution.py:18
  65.1 12.7 %psum.15 = f32[]{:T(128)} all-reduce(f32[]{:T(128)} %fusion.4), channel_id=1, replica_groups=mesh['groups'=2,'blk'=4,'rep'=2,'sub'=2] {'blk'}, use_global_device_ids=true, to_apply=%region_3.0 | all-reduce | flops 1 | bytes 8 | tf_op jit(solution)/shard_map/psum | solution.py:18
  78.4 0.0 copy-done.2
  78.5 0.0 copy-done.3
  78.5 0.0 copy-done
  78.5 0.8 fusion.3
  79.2 0.7 copy.9
  (1 shorter events, 0.0 us)
Async XLA Ops:
  7.2 26.0 %reduce-scatter.2.cloned.1.call-start = ((), (), s32[]{:S(2)}) async-start(), calls=%async_computation.1 | async-start | bytes 368640 | tf_op jit(solution)/shard_map/reduce_scatter | solution.py:14
  7.2 0.9 %copy-start.1 = (f32[8,4608]{1,0:T(8,128)S(1)}, f32[8,4608]{1,0:T(8,128)}, u32[]{:S(2)}) copy-start(f32[8,4608]{1,0:T(8,128)} %param.7) | copy-start | bytes 442372
  7.9 55.6 %all-reduce.2.cloned.1.call-start = ((), (), s32[]{:S(2)}) async-start(), calls=%async_computation.2 | async-start | bytes 147456 | tf_op jit(solution)/shard_map/psum | solution.py:17
  33.2 45.2 %copy-start.2 = (f32[8,4608]{1,0:T(8,128)S(1)}, f32[8,4608]{1,0:T(8,128)}, u32[]{:S(2)}) copy-start(f32[8,4608]{1,0:T(8,128)} %param.6) | copy-start | bytes 442372
  33.2 45.2 %copy-start.3 = (f32[8,4608]{1,0:T(8,128)S(1)}, f32[8,4608]{1,0:T(8,128)}, u32[]{:S(2)}) copy-start(f32[8,4608]{1,0:T(8,128)} %param.5) | copy-start | bytes 442372
  63.5 15.0 %copy-start = (bf16[8,4608]{1,0:T(8,128)(2,1)S(1)}, bf16[8,4608]{1,0:T(8,128)(2,1)}, u32[]{:S(2)}) copy-start(bf16[8,4608]{1,0:T(8,128)(2,1)} %all-reduce.2.cloned.1.call-done) | copy-start | bytes 221188
Sparse Core Ops, SparseCore 0:
  10.2 22.9 reduce-scatter.1
  35.5 27.9 all-reduce.1
where the time goes:
time: 87 us; the launch traced here: 86.8 us
  waiting for transfers between devices  41.9 us (48%)
  blocking collectives  26.8 us (31%)
  between operations  14.8 us (17%)
  other arithmetic  2.36 us (3%)
  local copies, waits for them, and re-layouts  0.91 us (1%)
    reduce_scatter x1, waiting for transfers between devices, per_device(): lax.psum_scatter(own_delta.astype(jnp.float32).astype(jnp.bfloat16), 'blk...  25.1 us
    psum x1, waiting for transfers between devices, per_device(): summed = lax.psum(share_sum, ('rep', 'sub')).astype(jnp.float32)  16.1 us
    all_gather x1, blocking collectives, per_device(): lax.all_gather(prev_master.astype(jnp.bfloat16), 'blk', axis=0, tiled=True)  14.1 us
    psum x1, blocking collectives, per_device(): squares = lax.psum(jnp.sum(summed * summed), 'blk')  12.7 us
  transfers between devices with their start and end apart: 2, of which 2 were waited for; matrix products, arithmetic and copies ran while one was open for 0% of the time, Pallas kernels for 0%

commit v1 on v0

--- a/solution.py
+++ b/solution.py
@@ -1,3 +1,4 @@
+import functools
 import jax
 import jax.numpy as jnp
 from jax import lax
@@ -7,6 +8,14 @@
 outer_rate = 0.7
 
 
+def serve_sections_here(xs, axis_name, named_axis):
+    main = lax.psum(lax.psum(xs, axis_name), axis_name=named_axis)
+    return main
+
+
+answer_the_joints = functools.partial(serve_sections_here, axis_name="rep", named_axis="sub")
+
+
 def per_device(replica_delta, momentum, params, prev_master):
     own_delta = replica_delta[0]
     width = own_delta.shape[1]
@@ -14,7 +23,7 @@
     share_sum = lax.psum_scatter(
         own_delta.astype(jnp.float32).astype(jnp.bfloat16), "blk", scatter_dimension=0, tiled=True
     )
-    summed = lax.psum(share_sum, ("rep", "sub")).astype(jnp.float32)
+    summed = answer_the_joints(share_sum).astype(jnp.float32)
     squares = lax.psum(jnp.sum(summed * summed), "blk")
     clip_factor = jnp.minimum(
         jnp.float32(1.0), jnp.sqrt(jnp.float32(entries)) / jnp.sqrt(squares + 1e-06)

time: 87 us -> 98 us (1.13)
  waiting for transfers between devices: 41.9 us -> 53.1 us
    psum x1 -> x2, waiting for transfers between devices: 16.1 us -> 27.2 us  [serve_sections_here(): main = lax.psum(lax.psum(xs, axis_name), axis_name=named_axis)]
  transfers between devices with their start and end apart: 2 -> 3, of which waited for: 2 -> 3; matrix products, arithmetic and copies ran while one was open for 0% -> 0% of each run, Pallas kernels for 0% -> 0%
where the time goes in v1:
time: 98 us; the launch traced here: 97.8 us
  waiting for transfers between devices  53.1 us (54%)
  blocking collectives  26.9 us (27%)
  between operations  14.5 us (15%)
  other arithmetic  2.36 us (2%)
    psum x2, waiting for transfers between devices, serve_sections_here(): main = lax.psum(lax.psum(xs, axis_name), axis_name=named_axis)  27.2 us
    reduce_scatter x1, waiting for transfers between devices, per_device(): lax.psum_scatter(own_delta.astype(jnp.float32).astype(jnp.bfloat16), 'blk...  25.3 us
    all_gather x1, blocking collectives, per_device(): lax.all_gather(prev_master.astype(jnp.bfloat16), 'blk', axis=0, tiled=True)  14.3 us
    psum x1, blocking collectives, per_device(): squares = lax.psum(jnp.sum(summed * summed), 'blk')  12.7 us
  transfers between devices with their start and end apart: 3, of which 3 were waited for; matrix products, arithmetic and copies ran while one was open for 0% of the time, Pallas kernels for 0%

profile of v1, /device:TPU:0, one launch (start us, length us, event | category | flops | bytes accessed | tf_op | source)
XLA Modules:
  0.0 97.8 jit_solution(17467676497439720712)
XLA Ops:
  7.2 0.0 reduce-scatter.2.cloned.1.call-start
  7.2 0.0 copy-start.1
  7.2 0.7 reduce-scatter.2.cloned.1.call-update
  7.9 0.0 all-reduce.3.cloned.1.call-start
  7.9 25.3 %reduce-scatter.2.cloned.1.call-done = bf16[8,4608]{1,0:T(8,128)(2,1)} async-done(((bf16[32,4608]{1,0:T(8,128)(2,1)}), bf16[8,4608]{1,0:T(8,128)(2,1)}) %reduce-scatter.2.cloned.1.call-update) | async-done | bytes 73744 | tf_op jit(solution)/shard_map/reduce_scatter | solution.py:23
  33.2 0.0 all-reduce.3.cloned.1.call-update
  33.2 0.0 all-reduce.5.cloned.1.call-start
  33.3 0.0 copy-done.1
  33.3 21.3 %all-reduce.3.cloned.1.call-done = bf16[8,4608]{1,0:T(8,128)(2,1)} async-done(((bf16[8,4608]{1,0:T(8,128)(2,1)}), bf16[8,4608]{1,0:T(8,128)(2,1)}) %all-reduce.3.cloned.1.call-update) | async-done | bytes 73744 | tf_op jit(solution)/shard_map/psum | solution.py:12
  54.6 0.0 all-reduce.5.cloned.1.call-update
  54.7 0.0 copy-start.2
  54.7 0.0 copy-start.3
  54.7 14.3 %all_gather.3 = bf16[32,4608]{1,0:T(8,128)(2,1)S(1)} all-gather(bf16[8,4608]{1,0:T(8,128)(2,1)S(1)} %convert_element_type.9), channel_id=1, replica_groups=mesh['groups'=2,'blk'=4,'rep'=2,'sub'=2] {'blk'}, dimensions={0}, use_global_device_ids=true | all-gather | bytes 368640 | tf_op jit(solution)/shard_map/all_gather | solution.py:34
  69.0 5.8 %all-reduce.5.cloned.1.call-done = bf16[8,4608]{1,0:T(8,128)(2,1)} async-done(((bf16[8,4608]{1,0:T(8,128)(2,1)}), bf16[8,4608]{1,0:T(8,128)(2,1)}) %all-reduce.5.cloned.1.call-update) | async-done | bytes 73744 | tf_op jit(solution)/shard_map/psum | solution.py:12
  74.8 0.0 copy-start
  74.8 1.6 %fusion.4 = f32[]{:T(128)} fusion(bf16[8,4608]{1,0:T(8,128)(2,1)} %all-reduce.5.cloned.1.call-done), kind=kLoop, calls=%fused_computation.6 | loop fusion | flops 110591 | bytes 73732 | tf_op jit(solution)/shard_map/reduce_sum | solution.py:27
  76.4 12.7 %psum.23 = f32[]{:T(128)} all-reduce(f32[]{:T(128)} %fusion.4), channel_id=1, replica_groups=mesh['groups'=2,'blk'=4,'rep'=2,'sub'=2] {'blk'}, use_global_device_ids=true, to_apply=%region_4.0 | all-reduce | flops 1 | bytes 8 | tf_op jit(solution)/shard_map/psum | solution.py:27
  89.8 0.0 copy-done.2
  89.8 0.0 copy-done.3
  89.8 0.0 copy-done
  89.8 0.8 fusion.3
  90.5 0.7 copy.10
  (1 shorter events, 0.0 us)
Async XLA Ops:
  7.2 26.0 %reduce-scatter.2.cloned.1.call-start = ((), (), s32[]{:S(2)}) async-start(), calls=%async_computation.1 | async-start | bytes 368640 | tf_op jit(solution)/shard_map/reduce_scatter | solution.py:23
  7.2 26.1 %copy-start.1 = (f32[8,4608]{1,0:T(8,128)S(1)}, f32[8,4608]{1,0:T(8,128)}, u32[]{:S(2)}) copy-start(f32[8,4608]{1,0:T(8,128)} %param.7) | copy-start | bytes 442372
  7.9 46.7 %all-reduce.3.cloned.1.call-start = ((), (), s32[]{:S(2)}) async-start(), calls=%async_computation.2 | async-start | bytes 147456 | tf_op jit(solution)/shard_map/psum | solution.py:12
  33.2 41.6 %all-reduce.5.cloned.1.call-start = ((), (), s32[]{:S(2)}) async-start(), calls=%async_computation.3 | async-start | bytes 147456 | tf_op jit(solution)/shard_map/psum | solution.py:12
  54.7 35.1 %copy-start.2 = (f32[8,4608]{1,0:T(8,128)S(1)}, f32[8,4608]{1,0:T(8,128)}, u32[]{:S(2)}) copy-start(f32[8,4608]{1,0:T(8,128)} %param.6) | copy-start | bytes 442372
  54.7 35.1 %copy-start.3 = (f32[8,4608]{1,0:T(8,128)S(1)}, f32[8,4608]{1,0:T(8,128)}, u32[]{:S(2)}) copy-start(f32[8,4608]{1,0:T(8,128)} %param.5) | copy-start | bytes 442372
  74.8 15.0 %copy-start = (bf16[8,4608]{1,0:T(8,128)(2,1)S(1)}, bf16[8,4608]{1,0:T(8,128)(2,1)}, u32[]{:S(2)}) copy-start(bf16[8,4608]{1,0:T(8,128)(2,1)} %all-reduce.5.cloned.1.call-done) | copy-start | bytes 221188
Sparse Core Ops, SparseCore 0:
  10.2 22.9 reduce-scatter.1
  35.4 19.1 all-reduce.2
  56.9 17.8 all-reduce.4

commit v2 on v0

--- a/solution.py
+++ b/solution.py
@@ -14,7 +14,8 @@
     share_sum = lax.psum_scatter(
         own_delta.astype(jnp.float32).astype(jnp.bfloat16), "blk", scatter_dimension=0, tiled=True
     )
-    summed = lax.psum(share_sum, ("rep", "sub")).astype(jnp.float32)
+    edit_state = lambda inputs: jnp.sum(lax.all_gather(inputs, ("rep", "sub")), axis=0)
+    summed = edit_state(share_sum).astype(jnp.float32)
     squares = lax.psum(jnp.sum(summed * summed), "blk")
     clip_factor = jnp.minimum(
         jnp.float32(1.0), jnp.sqrt(jnp.float32(entries)) / jnp.sqrt(squares + 1e-06)

time: 87 us -> 59.3 us (0.68)
  waiting for transfers between devices: 41.9 us -> 9.47 us
  blocking collectives: 26.8 us -> 32.4 us
  other arithmetic: 2.36 us -> 1.44 us
    reduce_scatter x1, waiting for transfers between devices: 25.1 us -> 8.8 us  [per_device(): lax.psum_scatter(own_delta.astype(jnp.float32).astype(jnp.bfloat16), 'blk...]
    psum x1 -> x0, waiting for transfers between devices: 16.1 us -> none  [per_device(): summed = lax.psum(share_sum, ('rep', 'sub')).astype(jnp.float32)]
    all_gather x0 -> x1, blocking collectives: none -> 6.08 us  [per_device(): lax.all_gather(inputs, ('rep', 'sub'))]
    psum x1, blocking collectives: 12.7 us -> 9.52 us  [per_device(): squares = lax.psum(jnp.sum(summed * summed), 'blk')]
    all_gather x1, blocking collectives: 14.1 us -> 16.8 us  [per_device(): lax.all_gather(prev_master.astype(jnp.bfloat16), 'blk', axis=0, tiled=True)]
    reduce_sum x1, other arithmetic: 1.6 us -> 0.64 us  [per_device(): squares = lax.psum(jnp.sum(summed * summed), 'blk')]
  transfers between devices with their start and end apart: 2 -> 1, of which waited for: 2 -> 1; matrix products, arithmetic and copies ran while one was open for 0% -> 0% of each run, Pallas kernels for 0% -> 0%
where the time goes in v2:
time: 59.3 us; the launch traced here: 59.1 us
  blocking collectives  32.4 us (55%)
  between operations  14.8 us (25%)
  waiting for transfers between devices  9.47 us (16%)
  other arithmetic  1.44 us (2%)
  local copies, waits for them, and re-layouts  0.95 us (2%)
    all_gather x1, blocking collectives, per_device(): lax.all_gather(prev_master.astype(jnp.bfloat16), 'blk', axis=0, tiled=True)  16.8 us
    psum x1, blocking collectives, per_device(): squares = lax.psum(jnp.sum(summed * summed), 'blk')  9.52 us
    reduce_scatter x1, waiting for transfers between devices, per_device(): lax.psum_scatter(own_delta.astype(jnp.float32).astype(jnp.bfloat16), 'blk...  8.8 us
    all_gather x1, blocking collectives, per_device(): lax.all_gather(inputs, ('rep', 'sub'))  6.08 us
  transfers between devices with their start and end apart: 1, of which 1 were waited for; matrix products, arithmetic and copies ran while one was open for 0% of the time, Pallas kernels for 0%

profile of v2, /device:TPU:0, one launch (start us, length us, event | category | flops | bytes accessed | tf_op | source)
XLA Modules:
  0.0 59.1 jit_solution(8711837118970726585)
XLA Ops:
  7.2 0.0 reduce-scatter.2.cloned.1.call-start
  7.2 0.0 copy-start
  7.2 0.7 %reduce-scatter.2.cloned.1.call-update = ((bf16[32,4608]{1,0:T(8,128)(2,1)}), bf16[8,4608]{1,0:T(8,128)(2,1)}) async-update(((), (), s32[]{:S(2)}) %reduce-scatter.2.cloned.1.call-start, bf16[32,4608]{1,0:T(8,128)(2,1)} %bitcast.3) | async-update | bytes 663576
  7.9 0.2 copy-done
  8.1 16.8 %all_gather.11 = bf16[32,4608]{1,0:T(8,128)(2,1)S(1)} all-gather(bf16[8,4608]{1,0:T(8,128)(2,1)S(1)} %convert_element_type.5), channel_id=1, replica_groups=mesh['groups'=2,'blk'=4,'rep'=2,'sub'=2] {'blk'}, dimensions={0}, use_global_device_ids=true | all-gather | bytes 368640 | tf_op jit(solution)/shard_map/all_gather | solution.py:26
  25.0 8.8 %reduce-scatter.2.cloned.1.call-done = bf16[8,4608]{1,0:T(8,128)(2,1)} async-done(((bf16[32,4608]{1,0:T(8,128)(2,1)}), bf16[8,4608]{1,0:T(8,128)(2,1)}) %reduce-scatter.2.cloned.1.call-update) | async-done | bytes 73744 | tf_op jit(solution)/shard_map/reduce_scatter | solution.py:14
  33.8 6.1 %all-gather = bf16[32,4608]{1,0:T(8,128)(2,1)S(1)} all-gather(bf16[8,4608]{1,0:T(8,128)(2,1)} %reduce-scatter.2.cloned.1.call-done), channel_id=2, replica_groups=mesh['groups'=2,'blk'=4,'rep'=2,'sub'=2] {'rep','sub'}, dimensions={0}, use_global_device_ids=true | all-gather | bytes 368640 | tf_op jit(solution)/shard_map/all_gather | solution.py:17
  39.8 0.0 copy-start.1
  39.8 0.0 copy-start.2
  39.9 0.6 %fusion.4 = f32[]{:T(128)} fusion(bf16[8,4608]{1,0:T(8,128)(2,1)S(1)} %bitcast_reduce_fusion), kind=kLoop, calls=%fused_computation.7 | loop fusion | flops 110591 | bytes 73732 | tf_op jit(solution)/shard_map/reduce_sum | solution.py:19
  40.5 9.5 %psum.7 = f32[]{:T(128)} all-reduce(f32[]{:T(128)} %fusion.4), channel_id=1, replica_groups=mesh['groups'=2,'blk'=4,'rep'=2,'sub'=2] {'blk'}, use_global_device_ids=true, to_apply=%region_3.0 | all-reduce | flops 1 | bytes 8 | tf_op jit(solution)/shard_map/psum | solution.py:19
  50.7 0.0 copy-done.1
  50.8 0.0 copy-done.2
  50.8 0.8 %fusion.3 = (f32[8,4608]{1,0:T(8,128)}, f32[8,4608]{1,0:T(8,128)}) fusion(f32[8,4608]{1,0:T(8,128)S(1)} %copy-done.1, bf16[8,4608]{1,0:T(8,128)(2,1)S(1)} %bitcast_reduce_fusion, f32[]{:T(128)S(6)} %min_shard_map.3, f32[8,4608]{1,0:T(8,128)S(1)} %copy-done.2), kind=kLoop, calls=%fused_computation.6 | loop fusion | flops 294912 | bytes 663556 | tf_op jit(solution)/shard_map/sub | solution.py:25
  51.5 0.7 %copy.8 = bf16[32,4608]{1,0:T(8,128)(2,1)} copy(bf16[32,4608]{1,0:T(8,128)(2,1)S(1)} %all_gather.11) | data formatting | bytes 589824
  (2 shorter events, 0.0 us)
Async XLA Ops:
  7.2 26.6 %reduce-scatter.2.cloned.1.call-start = ((), (), s32[]{:S(2)}) async-start(), calls=%async_computation.1 | async-start | bytes 368640 | tf_op jit(solution)/shard_map/reduce_scatter | solution.py:14
  7.2 0.9 %copy-start = (f32[8,4608]{1,0:T(8,128)S(1)}, f32[8,4608]{1,0:T(8,128)}, u32[]{:S(2)}) copy-start(f32[8,4608]{1,0:T(8,128)} %param.7) | copy-start | bytes 442372
  39.8 10.9 %copy-start.1 = (f32[8,4608]{1,0:T(8,128)S(1)}, f32[8,4608]{1,0:T(8,128)}, u32[]{:S(2)}) copy-start(f32[8,4608]{1,0:T(8,128)} %param.6) | copy-start | bytes 442372
  39.8 10.9 %copy-start.2 = (f32[8,4608]{1,0:T(8,128)S(1)}, f32[8,4608]{1,0:T(8,128)}, u32[]{:S(2)}) copy-start(f32[8,4608]{1,0:T(8,128)} %param.5) | copy-start | bytes 442372
Sparse Core Ops, SparseCore 0:
  10.2 23.4 reduce-scatter.1
